TPU v7x, 32 devices: a whole 2x2x4 slice. The times are simulated.
32 devices in a mesh: groups: 2 (over x), blk: 8 (over z, y), span: 2 (over core).
Axes of the slice: x: 2, y: 2, z: 4, core: 2. Of those that a mesh axis runs over, the one named last changes fastest.
Arguments:
- embeddings: bfloat16 [8192, 768], P(('groups', 'blk', 'span')), parts along dimension 0, may hold values from -6 to 6
- owner_ids: int32 [8192, 1], P(('groups', 'blk', 'span')), parts along dimension 0, may hold values from 0 to 7, as said below
- local_ids: int32 [8192], P(('groups', 'blk', 'span')), parts along dimension 0, may hold values from 0 to 15, as said below
- cluster_map: int32 [256], P('groups'), parts along dimension 0, may hold values from 0 to 127, as said below
Outputs:
- nearest: float32 [8192], P(('groups', 'blk', 'span')), parts along dimension 0
- centroid_cosine: float32 [8192], P(('groups', 'blk', 'span')), parts along dimension 0
There are 2 independent parts, one for each index of `groups`. A program takes and returns all parts, laid end to end along the dimension named above; each array names one. Nothing has to cross between parts.
Inputs may be any that keep to these rules, and one draw needn't show every extreme that they name: `owner_ids`: at most 64 rows of one device name the same owner; in every draw one owner is named by exactly 64 rows of every device. `local_ids`: of the rows of one device that name one owner, at most 16 have local id 0; in every draw one owner receives exactly 16 rows with local id 0 from every device. In every draw some clusters with a local id other than 0 have exactly one row in the whole shard. cluster_map[o * 16 + l] = o * 16 + l for l > 0. For l = 0 the owners fall into runs of 1 to 3 consecutive owners, and every owner of a run has the value of the run's first owner; some run has 3 owners.
All inputs are finite; a program needn't handle non-finite values.
Results may differ from a plain program's by a relative error of at most 0.0017.
Values may be sent and summed in bfloat16 or wider, within the bound.
No kernel may reach another device: no remote copies, remote signals or barrier semaphores. Data moves between devices by JAX's collectives and lax.ppermute only.
A program may use at most 64 MiB of HBM per device.

v0:
```python
import jax
import jax.numpy as jnp
from jax import lax
from jax.sharding import PartitionSpec as P

GIANT_SPAN = 3


def passed_along(value, axis, steps):
    count = lax.axis_size(axis)
    first, last = (max(0, -steps), min(count, count - steps))
    return lax.ppermute(value, axis, [(source, source + steps) for source in range(first, last)])


def normalize(values):
    wide = values.astype(jnp.float32)
    scale = lax.rsqrt(jnp.sum(wide * wide, axis=1, keepdims=True) + 1e-06)
    return (wide * scale).astype(jnp.bfloat16)


def masked_scores(left, left_tags, right, right_tags):
    scores = lax.dot_general(
        left, right, (((1,), (1,)), ((), ())), preferred_element_type=jnp.float32
    )
    same = (left_tags[:, None] == right_tags[None, :]) & (left_tags[:, None] > 0)
    return jnp.where(same, scores, -1.0)


def body(embeddings, owner_ids, local_ids, cluster_map):
    rows = embeddings.shape[0]
    width = embeddings.shape[1]
    owners = lax.axis_size("blk")
    capacity = 2 * rows // owners
    slots = owners * capacity
    clusters = cluster_map.shape[0]
    owned = clusters // owners
    unit = normalize(embeddings)
    destination = owner_ids[:, 0]
    flat = destination * owned + local_ids
    table = jnp.arange(clusters, dtype=jnp.int32)
    cluster = jnp.sum(jnp.where(flat[:, None] == table[None, :], cluster_map[None, :], 0), axis=1)
    onehot = (destination[:, None] == jnp.arange(owners, dtype=jnp.int32)[None, :]).astype(
        jnp.int32
    )
    before = jnp.cumsum(onehot, axis=0) - onehot
    rank = jnp.sum(before * onehot, axis=1)
    position = destination * capacity + rank
    send_rows = jnp.zeros((slots, width), jnp.bfloat16).at[position].set(unit)
    send_tags = jnp.zeros((slots,), jnp.int32).at[position].set(cluster + 1)
    arrived, arrived_tags = (
        lax.all_to_all(
            send_rows.reshape(owners, capacity, width),
            "blk",
            split_axis=0,
            concat_axis=0,
            tiled=True,
        ),
        lax.all_to_all(
            send_tags.reshape(owners, capacity), "blk", split_axis=0, concat_axis=0, tiled=True
        ),
    )
    mine = arrived.reshape(slots, width)
    my_tags = arrived_tags.reshape(slots)
    chip, chip_tags = (
        lax.all_gather(mine, "span", axis=0, tiled=True),
        lax.all_gather(my_tags, "span", axis=0, tiled=True),
    )
    half = lax.axis_index("span")
    block_index = lax.axis_index("blk")
    own_tags = lax.dynamic_slice_in_dim(cluster_map, block_index * owned, owned, 0) + 1
    local = masked_scores(mine, my_tags, chip, chip_tags)
    itself = (
        jnp.arange(2 * slots, dtype=jnp.int32)[None, :]
        == (jnp.arange(slots, dtype=jnp.int32) + half * slots)[:, None]
    )
    best = jnp.max(jnp.where(itself, -1.0, local), axis=1)
    share_limit = 2 * owners * max(1, capacity // 4)
    shared_mask = chip_tags == own_tags[0]
    packed_rank = jnp.cumsum(shared_mask.astype(jnp.int32)) - 1
    target = jnp.where(shared_mask, packed_rank, share_limit)
    packed = jnp.zeros((share_limit, width), jnp.bfloat16).at[target].set(chip, mode="drop")
    packed_tags = jnp.zeros((share_limit,), jnp.int32).at[target].set(chip_tags, mode="drop")
    upper = (packed, packed_tags)
    lower = (packed, packed_tags)
    for step in range(1, GIANT_SPAN):
        upper = passed_along((upper[0], upper[1]), "blk", 1)
        lower = passed_along((lower[0], lower[1]), "blk", -1)
        for other in (upper, lower):
            best = jnp.maximum(
                best, jnp.max(masked_scores(mine, my_tags, other[0], other[1]), axis=1)
            )
    chosen = cluster[:, None] == table[None, :]
    partial_sums = lax.dot_general(
        chosen.astype(jnp.bfloat16),
        unit,
        (((0,), (0,)), ((), ())),
        preferred_element_type=jnp.float32,
    )
    sums = lax.psum(partial_sums, ("blk", "span"))
    length = jnp.sqrt(jnp.sum(sums * sums, axis=1, keepdims=True))
    direction = sums / jnp.maximum(length, 1.0)
    centroid_cosine = jnp.sum(unit.astype(jnp.float32) * direction[cluster], axis=1)
    returned_best = lax.all_to_all(
        best.reshape(owners, capacity), "blk", split_axis=0, concat_axis=0, tiled=True
    )
    nearest = returned_best.reshape(slots)[position]
    return (nearest, centroid_cosine)


def solution(mesh):
    return jax.shard_map(
        body,
        mesh=mesh,
        in_specs=(
            P(("groups", "blk", "span"), None),
            P(("groups", "blk", "span"), None),
            P(("groups", "blk", "span")),
            P("groups"),
        ),
        out_specs=(P(("groups", "blk", "span")), P(("groups", "blk", "span"))),
        check_vma=False,
    )
```

profile of v0, /device:TPU:0, one launch (start us, length us, event | category | flops | bytes accessed | tf_op | source)
XLA Modules:
  0.0 191.0 jit_solution(9322189716579336675)
XLA Ops:
  8.0 1.2 fusion
  10.8 0.8 fusion.9
  12.2 3.1 %scatter_custom_fusion.1 = bf16[512,768]{1,0:T(8,128)(2,1)} fusion(s32[256]{0:T(256)S(1)} %bitcast.54, bf16[]{:T(256)} %constant.23.clone.1, bf16[256,768]{1,0:T(8,128)(2,1)} %param.4, f32[256]{0:T(256)S(1)} %add_rsqrt_fusion), kind=kCustom, calls=%fused_computation.18 | custom fusion | flops 589824 | bytes 1180674 | tf_op jit(solution)/shard_map/scatter | solution.py:48
  15.3 7.3 %all-to-all-start.1 = ((bf16[8,64,768]{2,1,0:T(8,128)(2,1)}), bf16[8,64,768]{2,1,0:T(8,128)(2,1)S(1)}, u32[]{:S(2)}, u32[]{:S(2)}) async-start(bf16[8,64,768]{2,1,0:T(8,128)(2,1)} %bitcast.7), calls=%async_computation.1 | async-start | bytes 1572864 | tf_op jit(solution)/shard_map/all_to_all | solution.py:51
  22.9 1.1 fusion.6
  24.1 1.4 scatter_custom_fusion
  26.7 16.9 %all-to-all-done.1 = bf16[8,64,768]{2,1,0:T(8,128)(2,1)S(1)} async-done(((bf16[8,64,768]{2,1,0:T(8,128)(2,1)}), bf16[8,64,768]{2,1,0:T(8,128)(2,1)S(1)}, u32[]{:S(2)}, u32[]{:S(2)}) %all-to-all-start.1) | async-done | bytes 786464 | tf_op jit(solution)/shard_map/all_to_all | solution.py:51
  43.6 3.5 %all-to-all-start = ((s32[8,1,64]{2,1,0:T(1,128)}), s32[8,1,64]{2,1,0:T(1,128)S(1)}, u32[]{:S(2)}, u32[]{:S(2)}) async-start(s32[8,1,64]{2,1,0:T(1,128)} %all_to_all.13), calls=%async_computation | async-start | bytes 8192 | tf_op jit(solution)/shard_map/all_to_all | solution.py:58
  48.3 5.2 %all-to-all-done = s32[8,1,64]{2,1,0:T(1,128)S(1)} async-done(((s32[8,1,64]{2,1,0:T(1,128)}), s32[8,1,64]{2,1,0:T(1,128)S(1)}, u32[]{:S(2)}, u32[]{:S(2)}) %all-to-all-start) | async-done | bytes 2080 | tf_op jit(solution)/shard_map/all_to_all | solution.py:58
  53.7 1.8 all-gather
  56.1 4.3 %scatter_custom_fusion.2 = s32[256]{0:T(256)S(1)} fusion(s32[1024]{0:T(1024)S(1)} %compare_select_fusion, s32[1024]{0:T(1024)S(1)} %bitcast.49, s32[]{:T(128)} %constant.19.clone.1), kind=kCustom, calls=%fused_computation.53 | custom fusion | bytes 1028 | tf_op jit(solution)/shard_map/scatter | solution.py:82
  60.4 1.3 collective-permute-start.2
  61.7 5.1 %collective-permute-start = (s32[256]{0:T(256)S(1)}, s32[256]{0:T(256)}, u32[]{:S(2)}, u32[]{:S(2)}) collective-permute-start(s32[256]{0:T(256)S(1)} %scatter_custom_fusion.2), channel_id=1, source_target_pairs={{0,2},{2,4},{4,6},{6,8},{8,10},{10,12},{12,14},{1,3},{3,5},{5,7},{... | collective-permute-start | bytes 3080 | tf_op jit(solution)/shard_map/ppermute | solution.py:12
  68.6 1.3 collective-permute-start.6
  69.9 5.1 %collective-permute-start.4 = (s32[256]{0:T(256)}, s32[256]{0:T(256)}, u32[]{:S(2)}, u32[]{:S(2)}) collective-permute-start(s32[256]{0:T(256)} %collective-permute-done), channel_id=1, source_target_pairs={{0,2},{2,4},{4,6},{6,8},{8,10},{10,12},{12,14},{1,3},{3,5},{5,7},{... | collective-permute-start | bytes 3080 | tf_op jit(solution)/shard_map/ppermute | solution.py:12
  75.0 47.2 %all-reduce.2.cloned.1.call-done = f32[128,768]{1,0:T(8,128)} async-done(((f32[128,768]{1,0:T(8,128)}), f32[128,768]{1,0:T(8,128)}) %all-reduce.2.cloned.1.call-update) | async-done | bytes 393232 | tf_op jit(solution)/shard_map/psum | solution.py:99
  122.2 1.1 multiply_reduce_fusion.1
  123.4 5.7 %scatter_custom_fusion.3 = bf16[256,768]{1,0:T(8,128)(2,1)S(1)} fusion(s32[1024]{0:T(1024)S(1)} %compare_select_fusion, bf16[1024,768]{1,0:T(8,128)(2,1)} %all-gather.3.cloned.1.call-done, bf16[]{:T(256)} %constant.23.clone.1), kind=kCustom, calls=%fused_computation.21 | custom fusion | bytes 393728 | tf_op jit(solution)/shard_map/scatter | solution.py:81
  129.1 1.3 collective-permute-start.3
  130.4 4.6 %collective-permute-start.1 = (bf16[256,768]{1,0:T(8,128)(2,1)S(1)}, bf16[256,768]{1,0:T(8,128)(2,1)S(1)}, u32[]{:S(2)}, u32[]{:S(2)}) collective-permute-start(bf16[256,768]{1,0:T(8,128)(2,1)S(1)} %scatter_custom_fusion.3), channel_id=1, source_target_pairs={{0,2},{2,4},{4,6},{6,8},{8,10},{10,12},{12,14},{1,3},{3,5},{5,7},{... | collective-permute-start | bytes 1179656 | tf_op jit(solution)/shard_map/ppermute | solution.py:12
  135.0 1.1 broadcast_divide_fusion
  136.1 1.4 gather_fusion.1
  137.5 2.8 %select_reduce_fusion = f32[512]{0:T(512)S(1)} fusion(bf16[512,768]{1,0:T(8,128)(2,1)S(1)} %bitcast.41, bf16[1024,768]{1,0:T(8,128)(2,1)} %all-gather.3.cloned.1.call-done, s32[1024]{0:T(1024)S(1)} %bitcast.50, s32[512]{0:T(512)} %iota_add_fusion, s32[512]{0:T(512)S(1)} %eq.145, pred[512]{0:T(512)(128)(4,1)} %broadcast_compare_fusion.1), kind=kOutput, calls=%fused_computation.6 | convolution fusion | flops 808451584 | bytes 2370048 | tf_op jit(solution)/shard_map/dot_general | solution.py:22
  141.0 1.3 collective-permute-start.7
  142.3 6.2 %collective-permute-done.1 = bf16[256,768]{1,0:T(8,128)(2,1)S(1)} collective-permute-done((bf16[256,768]{1,0:T(8,128)(2,1)S(1)}, bf16[256,768]{1,0:T(8,128)(2,1)S(1)}, u32[]{:S(2)}, u32[]{:S(2)}) %collective-permute-start.1) | collective-permute-done | bytes 393248 | tf_op jit(solution)/shard_map/ppermute | solution.py:12
  148.5 4.4 %collective-permute-start.5 = (bf16[256,768]{1,0:T(8,128)(2,1)S(1)}, bf16[256,768]{1,0:T(8,128)(2,1)S(1)}, u32[]{:S(2)}, u32[]{:S(2)}) collective-permute-start(bf16[256,768]{1,0:T(8,128)(2,1)S(1)} %collective-permute-done.1), channel_id=1, source_target_pairs={{0,2},{2,4},{4,6},{6,8},{8,10},{10,12},{12,14},{1,3},{3,5},{5,7},{... | collective-permute-start | bytes 1179656 | tf_op jit(solution)/shard_map/ppermute | solution.py:12
  154.1 11.3 %collective-permute-done.5 = bf16[256,768]{1,0:T(8,128)(2,1)S(1)} collective-permute-done((bf16[256,768]{1,0:T(8,128)(2,1)S(1)}, bf16[256,768]{1,0:T(8,128)(2,1)S(1)}, u32[]{:S(2)}, u32[]{:S(2)}) %collective-permute-start.5) | collective-permute-done | bytes 393248 | tf_op jit(solution)/shard_map/ppermute | solution.py:12
  165.4 1.3 select_reduce_fusion.4
  167.4 5.9 %all-to-all-start.2 = ((f32[8,1,64]{2,1,0:T(1,128)}), f32[8,1,64]{2,1,0:T(1,128)S(1)}, u32[]{:S(2)}, u32[]{:S(2)}) async-start(f32[8,1,64]{2,1,0:T(1,128)} %max.65), calls=%async_computation.2 | async-start | bytes 8192 | tf_op jit(solution)/shard_map/all_to_all | solution.py:103
  173.3 0.8 multiply_reduce_fusion
  174.1 5.7 %all-to-all-done.2 = f32[8,1,64]{2,1,0:T(1,128)S(1)} async-done(((f32[8,1,64]{2,1,0:T(1,128)}), f32[8,1,64]{2,1,0:T(1,128)S(1)}, u32[]{:S(2)}, u32[]{:S(2)}) %all-to-all-start.2) | async-done | bytes 2080 | tf_op jit(solution)/shard_map/all_to_all | solution.py:103
  181.1 2.5 %gather_fusion = f32[256]{0:T(256)} fusion(f32[512]{0:T(512)S(1)} %reshape.165, s32[1024]{0:T(1024)S(1)} %pad_clamp_fusion.1), kind=kCustom, calls=%fused_computation | custom fusion | bytes 3072 | tf_op jit(solution)/shard_map/gather | solution.py:106
  (61 shorter events, 11.3 us)
Async XLA Ops:
  8.0 14.9 %copy-start.2 = (bf16[256,768]{1,0:T(8,128)(2,1)S(1)}, bf16[256,768]{1,0:T(8,128)(2,1)}, u32[]{:S(2)}) copy-start(bf16[256,768]{1,0:T(8,128)(2,1)} %param.4) | copy-start | bytes 1179652
  8.0 14.7 %copy-start.3 = (s32[256,1]{0,1:T(1,128)S(1)}, s32[256,1]{0,1:T(1,128)}, u32[]{:S(2)}) copy-start(s32[256,1]{0,1:T(1,128)} %param.5) | copy-start | bytes 3076
  8.0 14.7 %copy-start.4 = (s32[256]{0:T(256)S(1)}, s32[256]{0:T(256)}, u32[]{:S(2)}) copy-start(s32[256]{0:T(256)} %param.6) | copy-start | bytes 3076
  8.0 14.7 %copy-start.5 = (s32[128]{0:T(128)S(1)}, s32[128]{0:T(128)}, u32[]{:S(2)}) copy-start(s32[128]{0:T(128)} %param.7) | copy-start | bytes 1540
  15.3 28.3 %all-to-all-start.1 = ((bf16[8,64,768]{2,1,0:T(8,128)(2,1)}), bf16[8,64,768]{2,1,0:T(8,128)(2,1)S(1)}, u32[]{:S(2)}, u32[]{:S(2)}) async-start(bf16[8,64,768]{2,1,0:T(8,128)(2,1)} %bitcast.7), calls=%async_computation.1 | async-start | bytes 1572864 | tf_op jit(solution)/shard_map/all_to_all | solution.py:51
  22.6 99.6 %all-reduce.2.cloned.1.call-start = ((), (), s32[]{:S(2)}) async-start(), calls=%async_computation.4 | async-start | bytes 786432 | tf_op jit(solution)/shard_map/psum | solution.py:99
  43.6 3.5 %copy-start = (bf16[8,64,768]{2,1,0:T(8,128)(2,1)}, bf16[8,64,768]{2,1,0:T(8,128)(2,1)S(1)}, u32[]{:S(2)}) copy-start(bf16[8,64,768]{2,1,0:T(8,128)(2,1)S(1)} %all-to-all-done.1) | copy-start | bytes 2359300
  43.6 10.0 %all-to-all-start = ((s32[8,1,64]{2,1,0:T(1,128)}), s32[8,1,64]{2,1,0:T(1,128)S(1)}, u32[]{:S(2)}, u32[]{:S(2)}) async-start(s32[8,1,64]{2,1,0:T(1,128)} %all_to_all.13), calls=%async_computation | async-start | bytes 8192 | tf_op jit(solution)/shard_map/all_to_all | solution.py:58
  47.1 76.3 %all-gather.3.cloned.1.call-start = ((), (), s32[]{:S(2)}) async-start(), calls=%async_computation.3 | async-start | bytes 2359296 | tf_op jit(solution)/shard_map/all_gather | solution.py:65
  60.4 8.2 %collective-permute-start.2 = (s32[256]{0:T(256)S(1)}, s32[256]{0:T(256)}, u32[]{:S(2)}, u32[]{:S(2)}) collective-permute-start(s32[256]{0:T(256)S(1)} %scatter_custom_fusion.2), channel_id=1, source_target_pairs={{2,0},{4,2},{6,4},{8,6},{10,8},{12,10},{14,12},{3,1},{5,3},{7,5},{... | collective-permute-start | bytes 3080 | tf_op jit(solution)/shard_map/ppermute | solution.py:12
  61.7 8.2 %collective-permute-start = (s32[256]{0:T(256)S(1)}, s32[256]{0:T(256)}, u32[]{:S(2)}, u32[]{:S(2)}) collective-permute-start(s32[256]{0:T(256)S(1)} %scatter_custom_fusion.2), channel_id=1, source_target_pairs={{0,2},{2,4},{4,6},{6,8},{8,10},{10,12},{12,14},{1,3},{3,5},{5,7},{... | collective-permute-start | bytes 3080 | tf_op jit(solution)/shard_map/ppermute | solution.py:12
  68.6 85.5 %collective-permute-start.6 = (s32[256]{0:T(256)}, s32[256]{0:T(256)}, u32[]{:S(2)}, u32[]{:S(2)}) collective-permute-start(s32[256]{0:T(256)} %collective-permute-done.2), channel_id=1, source_target_pairs={{2,0},{4,2},{6,4},{8,6},{10,8},{12,10},{14,12},{3,1},{5,3},{7,5},{... | collective-permute-start | bytes 3080 | tf_op jit(solution)/shard_map/ppermute | solution.py:12
  69.9 84.3 %collective-permute-start.4 = (s32[256]{0:T(256)}, s32[256]{0:T(256)}, u32[]{:S(2)}, u32[]{:S(2)}) collective-permute-start(s32[256]{0:T(256)} %collective-permute-done), channel_id=1, source_target_pairs={{0,2},{2,4},{4,6},{6,8},{8,10},{10,12},{12,14},{1,3},{3,5},{5,7},{... | collective-permute-start | bytes 3080 | tf_op jit(solution)/shard_map/ppermute | solution.py:12
  129.1 11.9 %collective-permute-start.3 = (bf16[256,768]{1,0:T(8,128)(2,1)S(1)}, bf16[256,768]{1,0:T(8,128)(2,1)S(1)}, u32[]{:S(2)}, u32[]{:S(2)}) collective-permute-start(bf16[256,768]{1,0:T(8,128)(2,1)S(1)} %scatter_custom_fusion.3), channel_id=1, source_target_pairs={{2,0},{4,2},{6,4},{8,6},{10,8},{12,10},{14,12},{3,1},{5,3},{7,5},{... | collective-permute-start | bytes 1179656 | tf_op jit(solution)/shard_map/ppermute | solution.py:12
  130.4 18.0 %collective-permute-start.1 = (bf16[256,768]{1,0:T(8,128)(2,1)S(1)}, bf16[256,768]{1,0:T(8,128)(2,1)S(1)}, u32[]{:S(2)}, u32[]{:S(2)}) collective-permute-start(bf16[256,768]{1,0:T(8,128)(2,1)S(1)} %scatter_custom_fusion.3), channel_id=1, source_target_pairs={{0,2},{2,4},{4,6},{6,8},{8,10},{10,12},{12,14},{1,3},{3,5},{5,7},{... | collective-permute-start | bytes 1179656 | tf_op jit(solution)/shard_map/ppermute | solution.py:12
  136.1 1.4 copy-start.1
  141.0 12.7 %collective-permute-start.7 = (bf16[256,768]{1,0:T(8,128)(2,1)S(1)}, bf16[256,768]{1,0:T(8,128)(2,1)S(1)}, u32[]{:S(2)}, u32[]{:S(2)}) collective-permute-start(bf16[256,768]{1,0:T(8,128)(2,1)S(1)} %collective-permute-done.3), channel_id=1, source_target_pairs={{2,0},{4,2},{6,4},{8,6},{10,8},{12,10},{14,12},{3,1},{5,3},{7,5},{... | collective-permute-start | bytes 1179656 | tf_op jit(solution)/shard_map/ppermute | solution.py:12
  148.5 17.0 %collective-permute-start.5 = (bf16[256,768]{1,0:T(8,128)(2,1)S(1)}, bf16[256,768]{1,0:T(8,128)(2,1)S(1)}, u32[]{:S(2)}, u32[]{:S(2)}) collective-permute-start(bf16[256,768]{1,0:T(8,128)(2,1)S(1)} %collective-permute-done.1), channel_id=1, source_target_pairs={{0,2},{2,4},{4,6},{6,8},{8,10},{10,12},{12,14},{1,3},{3,5},{5,7},{... | collective-permute-start | bytes 1179656 | tf_op jit(solution)/shard_map/ppermute | solution.py:12
  153.3 12.2 %copy-start.6 = (pred[512]{0:T(512)(128)(4,1)S(1)}, pred[512]{0:T(512)(128)(4,1)}, u32[]{:S(2)}) copy-start(pred[512]{0:T(512)(128)(4,1)} %broadcast_compare_fusion.1) | copy-start | bytes 1540
  167.4 12.4 %all-to-all-start.2 = ((f32[8,1,64]{2,1,0:T(1,128)}), f32[8,1,64]{2,1,0:T(1,128)S(1)}, u32[]{:S(2)}, u32[]{:S(2)}) async-start(f32[8,1,64]{2,1,0:T(1,128)} %max.65), calls=%async_computation.2 | async-start | bytes 8192 | tf_op jit(solution)/shard_map/all_to_all | solution.py:103
Sparse Core Ops, SparseCore 0:
  26.8 95.4 all-reduce.1
Sparse Core Ops, SparseCore 1:
  49.1 11.1 all-gather.2
where the time goes:
time: 192 us; the launch traced here: 191 us
  waiting for transfers between devices  93.8 us (49%)
  starting transfers between devices  41.1 us (21%)
  local copies, waits for them, and re-layouts  18.3 us (10%)
  between operations  15.8 us (8%)
  other arithmetic  13.8 us (7%)
  matrix products  6.34 us (3%)
    psum x1, waiting for transfers between devices, body(): sums = lax.psum(partial_sums, ('blk', 'span'))  47.2 us
    ppermute x8, starting transfers between devices, passed_along(): lax.ppermute(value, axis, [(source, source + steps) for source in range(f...  24.3 us
    ppermute x8, waiting for transfers between devices, passed_along(): lax.ppermute(value, axis, [(source, source + steps) for source in range(f...  18.2 us
    all_to_all x1, waiting for transfers between devices, body(): lax.all_to_all(send_rows.reshape(owners, capacity, width), 'blk', split_a...  16.9 us
    all_to_all x1, starting transfers between devices, body(): lax.all_to_all(send_rows.reshape(owners, capacity, width), 'blk', split_a...  7.31 us
    all_to_all x1, starting transfers between devices, body(): lax.all_to_all(best.reshape(owners, capacity), 'blk', split_axis=0, conca...  5.92 us
    scatter x1, local copies, waits for them, and re-layouts, body(): jnp.zeros((share_limit, width), jnp.bfloat16).at[target]  5.74 us
    all_to_all x1, waiting for transfers between devices, body(): lax.all_to_all(best.reshape(owners, capacity), 'blk', split_axis=0, conca...  5.68 us
  transfers between devices with their start and end apart: 13, of which 7 were waited for; matrix products, arithmetic and copies ran while one was open for 13% of the time, Pallas kernels for 0%

commit v1 on v0

--- a/solution.py
+++ b/solution.py
@@ -96,7 +96,7 @@
         (((0,), (0,)), ((), ())),
         preferred_element_type=jnp.float32,
     )
-    sums = lax.psum(partial_sums, ("blk", "span"))
+    sums = jnp.sum(lax.all_gather(partial_sums, ("blk", "span")), axis=0)
     length = jnp.sqrt(jnp.sum(sums * sums, axis=1, keepdims=True))
     direction = sums / jnp.maximum(length, 1.0)
     centroid_cosine = jnp.sum(unit.astype(jnp.float32) * direction[cluster], axis=1)

time: 192 us -> 157 us (0.82)
  waiting for transfers between devices: 93.8 us -> 45.6 us
  blocking collectives: 1.83 us -> 29.2 us
  starting transfers between devices: 41.1 us -> 30.9 us
    psum x1 -> x0, waiting for transfers between devices: 47.2 us -> none  [body(): sums = lax.psum(partial_sums, ('blk', 'span'))]
    all_to_all x0 -> x1, blocking collectives: none -> 27.4 us  [body(): lax.all_to_all(send_rows.reshape(owners, capacity, width), 'blk', split_a...]
    all_to_all x1 -> x0, waiting for transfers between devices: 16.9 us -> none  [body(): lax.all_to_all(send_rows.reshape(owners, capacity, width), 'blk', split_a...]
    ppermute x8, waiting for transfers between devices: 18.2 us -> 32.7 us  [passed_along(): lax.ppermute(value, axis, [(source, source + steps) for source in range(f...]
    all_to_all x1 -> x0, starting transfers between devices: 7.31 us -> none  [body(): lax.all_to_all(send_rows.reshape(owners, capacity, width), 'blk', split_a...]
    reduce_sum x0 -> x1, other arithmetic: none -> 3.18 us  [body(): sums = jnp.sum(lax.all_gather(partial_sums, ('blk', 'span')), axis=0)]
  transfers between devices with their start and end apart: 13 -> 12, of which waited for: 7 -> 4; matrix products, arithmetic and copies ran while one was open for 13% -> 15% of each run, Pallas kernels for 0% -> 0%
where the time goes in v1:
time: 157 us; the launch traced here: 156 us
  waiting for transfers between devices  45.6 us (29%)
  starting transfers between devices  30.9 us (20%)
  blocking collectives  29.2 us (19%)
  local copies, waits for them, and re-layouts  18.1 us (12%)
  between operations  14.4 us (9%)
  other arithmetic  12.6 us (8%)
  matrix products  5.67 us (4%)
    ppermute x8, waiting for transfers between devices, passed_along(): lax.ppermute(value, axis, [(source, source + steps) for source in range(f...  32.7 us
    all_to_all x1, blocking collectives, body(): lax.all_to_all(send_rows.reshape(owners, capacity, width), 'blk', split_a...  27.4 us
    ppermute x8, starting transfers between devices, passed_along(): lax.ppermute(value, axis, [(source, source + steps) for source in range(f...  22.7 us
    all_to_all x1, waiting for transfers between devices, body(): lax.all_to_all(best.reshape(owners, capacity), 'blk', split_axis=0, conca...  6.49 us
    all_to_all x1, waiting for transfers between devices, body(): lax.all_to_all(send_tags.reshape(owners, capacity), 'blk', split_axis=0,...  6.38 us
    scatter x1, local copies, waits for them, and re-layouts, body(): jnp.zeros((share_limit, width), jnp.bfloat16).at[target]  5.73 us
    all_to_all x1, starting transfers between devices, body(): lax.all_to_all(best.reshape(owners, capacity), 'blk', split_axis=0, conca...  4.57 us
    dot_general x5, matrix products, masked_scores(): lax.dot_general(left, right, (((1,), (1,)), ((), ())), preferred_element_...  4.56 us
  transfers between devices with their start and end apart: 12, of which 4 were waited for; matrix products, arithmetic and copies ran while one was open for 15% of the time, Pallas kernels for 0%

profile of v1, /device:TPU:0, one launch (start us, length us, event | category | flops | bytes accessed | tf_op | source)
XLA Modules:
  0.0 156.5 jit_solution(11686574984620200246)
XLA Ops:
  7.3 0.7 fusion.10
  8.8 0.8 fusion.9
  9.6 0.7 compare_select_fusion.2
  10.3 1.2 fusion
  11.4 2.4 %scatter_custom_fusion.1 = bf16[512,768]{1,0:T(8,128)(2,1)S(1)} fusion(s32[256]{0:T(256)S(1)} %bitcast.53, bf16[]{:T(256)} %constant.23.clone.1, bf16[256,768]{1,0:T(8,128)(2,1)} %param.4, f32[256]{0:T(256)S(1)} %add_rsqrt_fusion), kind=kCustom, calls=%fused_computation.18 | custom fusion | flops 589824 | bytes 1180674 | tf_op jit(solution)/shard_map/scatter | solution.py:48
  13.9 27.4 %all_to_all.20 = bf16[8,64,768]{2,1,0:T(8,128)(2,1)} all-to-all(bf16[8,64,768]{2,1,0:T(8,128)(2,1)S(1)} %bitcast.44), channel_id=1, replica_groups=mesh['groups'=2,'blk'=8,'span'=2] {'blk'}, dimensions={0} | all-to-all | bytes 1572864 | tf_op jit(solution)/shard_map/all_to_all | solution.py:51
  41.5 1.1 fusion.6
  42.7 1.4 scatter_custom_fusion
  44.1 0.7 all_to_all.13
  44.7 3.6 %all-to-all-start = ((s32[8,1,64]{2,1,0:T(1,128)}), s32[8,1,64]{2,1,0:T(1,128)S(1)}, u32[]{:S(2)}, u32[]{:S(2)}) async-start(s32[8,1,64]{2,1,0:T(1,128)} %all_to_all.13), calls=%async_computation | async-start | bytes 8192 | tf_op jit(solution)/shard_map/all_to_all | solution.py:58
  48.4 6.4 %all-to-all-done = s32[8,1,64]{2,1,0:T(1,128)S(1)} async-done(((s32[8,1,64]{2,1,0:T(1,128)}), s32[8,1,64]{2,1,0:T(1,128)S(1)}, u32[]{:S(2)}, u32[]{:S(2)}) %all-to-all-start) | async-done | bytes 2080 | tf_op jit(solution)/shard_map/all_to_all | solution.py:58
  54.9 1.8 %all-gather.1 = s32[2,1,512]{2,1,0:T(1,128)S(1)} all-gather(s32[1,1,512]{2,1,0:T(1,128)S(1)} %reshape.218), channel_id=1, replica_groups=mesh['groups'=2,'blk'=8,'span'=2] {'span'}, dimensions={0}, use_global_device_ids=true | all-gather | bytes 6144 | tf_op jit(solution)/shard_map/all_gather | solution.py:66
  57.4 4.3 %scatter_custom_fusion.2 = s32[256]{0:T(256)S(1)} fusion(s32[1024]{0:T(1024)S(1)} %compare_select_fusion, s32[1024]{0:T(1024)S(1)} %bitcast.48, s32[]{:T(128)} %constant.19.clone.1), kind=kCustom, calls=%fused_computation.53 | custom fusion | bytes 1028 | tf_op jit(solution)/shard_map/scatter | solution.py:82
  61.7 2.5 %collective-permute-start = (s32[256]{0:T(256)S(1)}, s32[256]{0:T(256)S(1)}, u32[]{:S(2)}, u32[]{:S(2)}) collective-permute-start(s32[256]{0:T(256)S(1)} %scatter_custom_fusion.2), channel_id=1, source_target_pairs={{0,2},{2,4},{4,6},{6,8},{8,10},{10,12},{12,14},{1,3},{3,5},{5,7},{... | collective-permute-start | bytes 3080 | tf_op jit(solution)/shard_map/ppermute | solution.py:12
  64.1 1.3 collective-permute-start.2
  66.7 5.7 %scatter_custom_fusion.3 = bf16[256,768]{1,0:T(8,128)(2,1)S(1)} fusion(s32[1024]{0:T(1024)S(1)} %compare_select_fusion, bf16[1024,768]{1,0:T(8,128)(2,1)} %all-gather.5.cloned.1.call-done, bf16[]{:T(256)} %constant.23.clone.1), kind=kCustom, calls=%fused_computation.21 | custom fusion | bytes 393728 | tf_op jit(solution)/shard_map/scatter | solution.py:81
  72.4 1.3 collective-permute-start.3
  73.7 5.2 %collective-permute-start.4 = (s32[256]{0:T(256)S(1)}, s32[256]{0:T(256)S(1)}, u32[]{:S(2)}, u32[]{:S(2)}) collective-permute-start(s32[256]{0:T(256)S(1)} %collective-permute-done), channel_id=1, source_target_pairs={{0,2},{2,4},{4,6},{6,8},{8,10},{10,12},{12,14},{1,3},{3,5},{5,7},{... | collective-permute-start | bytes 3080 | tf_op jit(solution)/shard_map/ppermute | solution.py:12
  78.9 1.3 collective-permute-start.6
  80.2 5.5 %collective-permute-start.1 = (bf16[256,768]{1,0:T(8,128)(2,1)S(1)}, bf16[256,768]{1,0:T(8,128)(2,1)S(1)}, u32[]{:S(2)}, u32[]{:S(2)}) collective-permute-start(bf16[256,768]{1,0:T(8,128)(2,1)S(1)} %scatter_custom_fusion.3), channel_id=1, source_target_pairs={{0,2},{2,4},{4,6},{6,8},{8,10},{10,12},{12,14},{1,3},{3,5},{5,7},{... | collective-permute-start | bytes 1179656 | tf_op jit(solution)/shard_map/ppermute | solution.py:12
  85.7 2.8 %select_reduce_fusion = f32[512]{0:T(512)S(1)} fusion(bf16[512,768]{1,0:T(8,128)(2,1)S(1)} %bitcast.38, bf16[1024,768]{1,0:T(8,128)(2,1)} %all-gather.5.cloned.1.call-done, s32[1024]{0:T(1024)S(1)} %bitcast.49, s32[512]{0:T(512)S(1)} %iota_add_fusion, s32[512]{0:T(512)S(1)} %eq.145, pred[512]{0:T(512)(128)(4,1)S(1)} %broadcast_compare_fusion.1), kind=kOutput, calls=%fused_computation.6 | convolution fusion | flops 808451584 | bytes 2370048 | tf_op jit(solution)/shard_map/dot_general | solution.py:22
  88.5 1.3 collective-permute-start.7
  90.2 22.4 %collective-permute-done.1 = bf16[256,768]{1,0:T(8,128)(2,1)S(1)} collective-permute-done((bf16[256,768]{1,0:T(8,128)(2,1)S(1)}, bf16[256,768]{1,0:T(8,128)(2,1)S(1)}, u32[]{:S(2)}, u32[]{:S(2)}) %collective-permute-start.1) | collective-permute-done | bytes 393248 | tf_op jit(solution)/shard_map/ppermute | solution.py:12
  112.7 4.4 %collective-permute-start.5 = (bf16[256,768]{1,0:T(8,128)(2,1)S(1)}, bf16[256,768]{1,0:T(8,128)(2,1)S(1)}, u32[]{:S(2)}, u32[]{:S(2)}) collective-permute-start(bf16[256,768]{1,0:T(8,128)(2,1)S(1)} %collective-permute-done.1), channel_id=1, source_target_pairs={{0,2},{2,4},{4,6},{6,8},{8,10},{10,12},{12,14},{1,3},{3,5},{5,7},{... | collective-permute-start | bytes 1179656 | tf_op jit(solution)/shard_map/ppermute | solution.py:12
  117.9 10.3 %collective-permute-done.5 = bf16[256,768]{1,0:T(8,128)(2,1)S(1)} collective-permute-done((bf16[256,768]{1,0:T(8,128)(2,1)S(1)}, bf16[256,768]{1,0:T(8,128)(2,1)S(1)}, u32[]{:S(2)}, u32[]{:S(2)}) %collective-permute-start.5) | collective-permute-done | bytes 393248 | tf_op jit(solution)/shard_map/ppermute | solution.py:12
  128.8 0.7 max.65
  129.5 4.6 %all-to-all-start.2 = ((f32[8,1,64]{2,1,0:T(1,128)}), f32[8,1,64]{2,1,0:T(1,128)S(1)}, u32[]{:S(2)}, u32[]{:S(2)}) async-start(f32[8,1,64]{2,1,0:T(1,128)} %max.65), calls=%async_computation.2 | async-start | bytes 8192 | tf_op jit(solution)/shard_map/all_to_all | solution.py:103
  134.0 6.5 %all-to-all-done.2 = f32[8,1,64]{2,1,0:T(1,128)S(1)} async-done(((f32[8,1,64]{2,1,0:T(1,128)}), f32[8,1,64]{2,1,0:T(1,128)S(1)}, u32[]{:S(2)}, u32[]{:S(2)}) %all-to-all-start.2) | async-done | bytes 2080 | tf_op jit(solution)/shard_map/all_to_all | solution.py:103
  141.8 2.5 %gather_fusion = f32[256]{0:T(256)} fusion(f32[512]{0:T(512)S(1)} %reshape.165, s32[1024]{0:T(1024)S(1)} %pad_clamp_fusion.1), kind=kCustom, calls=%fused_computation | custom fusion | bytes 3072 | tf_op jit(solution)/shard_map/gather | solution.py:106
  144.3 3.2 %reduce_sum.62 = f32[128,768]{1,0:T(8,128)S(1)} reduce(f32[16,128,768]{2,1,0:T(8,128)} %bitcast.43, f32[]{:T(128)} %constant.24.clone.1), dimensions={0}, to_apply=%region_16.17 | reduce | flops 1474560 | bytes 6684676 | tf_op jit(solution)/shard_map/reduce_sum | solution.py:99
  147.7 1.1 gather_fusion.1
  148.8 0.8 multiply_reduce_fusion
  (57 shorter events, 6.5 us)
Async XLA Ops:
  7.2 34.1 %copy-start.2 = (s32[256,1]{0,1:T(1,128)S(1)}, s32[256,1]{0,1:T(1,128)}, u32[]{:S(2)}) copy-start(s32[256,1]{0,1:T(1,128)} %param.5) | copy-start | bytes 3076
  7.2 34.3 %copy-start.1 = (bf16[256,768]{1,0:T(8,128)(2,1)S(1)}, bf16[256,768]{1,0:T(8,128)(2,1)}, u32[]{:S(2)}) copy-start(bf16[256,768]{1,0:T(8,128)(2,1)} %param.4) | copy-start | bytes 1179652
  7.2 34.1 %copy-start.3 = (s32[256]{0:T(256)S(1)}, s32[256]{0:T(256)}, u32[]{:S(2)}) copy-start(s32[256]{0:T(256)} %param.6) | copy-start | bytes 3076
  7.2 34.1 %copy-start.4 = (s32[128]{0:T(128)S(1)}, s32[128]{0:T(128)}, u32[]{:S(2)}) copy-start(s32[128]{0:T(128)} %param.7) | copy-start | bytes 1540
  7.2 59.5 %all-gather.5.cloned.1.call-start = ((), (), s32[]{:S(2)}) async-start(), calls=%async_computation.3 | async-start | bytes 2359296 | tf_op jit(solution)/shard_map/all_gather | solution.py:65
  41.2 44.5 %copy-start = (bf16[8,64,768]{2,1,0:T(8,128)(2,1)S(1)}, bf16[8,64,768]{2,1,0:T(8,128)(2,1)}, u32[]{:S(2)}) copy-start(bf16[8,64,768]{2,1,0:T(8,128)(2,1)} %all_to_all.20) | copy-start | bytes 2359300
  41.2 103.0 %all-gather.7.cloned.1.call-start = ((), (), s32[]{:S(2)}) async-start(), calls=%async_computation.4 | async-start | bytes 6684672 | tf_op jit(solution)/shard_map/all_gather | solution.py:99
  44.7 10.1 %all-to-all-start = ((s32[8,1,64]{2,1,0:T(1,128)}), s32[8,1,64]{2,1,0:T(1,128)S(1)}, u32[]{:S(2)}, u32[]{:S(2)}) async-start(s32[8,1,64]{2,1,0:T(1,128)} %all_to_all.13), calls=%async_computation | async-start | bytes 8192 | tf_op jit(solution)/shard_map/all_to_all | solution.py:58
  61.7 12.1 %collective-permute-start = (s32[256]{0:T(256)S(1)}, s32[256]{0:T(256)S(1)}, u32[]{:S(2)}, u32[]{:S(2)}) collective-permute-start(s32[256]{0:T(256)S(1)} %scatter_custom_fusion.2), channel_id=1, source_target_pairs={{0,2},{2,4},{4,6},{6,8},{8,10},{10,12},{12,14},{1,3},{3,5},{5,7},{... | collective-permute-start | bytes 3080 | tf_op jit(solution)/shard_map/ppermute | solution.py:12
  64.1 14.8 %collective-permute-start.2 = (s32[256]{0:T(256)S(1)}, s32[256]{0:T(256)S(1)}, u32[]{:S(2)}, u32[]{:S(2)}) collective-permute-start(s32[256]{0:T(256)S(1)} %scatter_custom_fusion.2), channel_id=1, source_target_pairs={{2,0},{4,2},{6,4},{8,6},{10,8},{12,10},{14,12},{3,1},{5,3},{7,5},{... | collective-permute-start | bytes 3080 | tf_op jit(solution)/shard_map/ppermute | solution.py:12
  72.4 16.1 %collective-permute-start.3 = (bf16[256,768]{1,0:T(8,128)(2,1)S(1)}, bf16[256,768]{1,0:T(8,128)(2,1)S(1)}, u32[]{:S(2)}, u32[]{:S(2)}) collective-permute-start(bf16[256,768]{1,0:T(8,128)(2,1)S(1)} %scatter_custom_fusion.3), channel_id=1, source_target_pairs={{2,0},{4,2},{6,4},{8,6},{10,8},{12,10},{14,12},{3,1},{5,3},{7,5},{... | collective-permute-start | bytes 1179656 | tf_op jit(solution)/shard_map/ppermute | solution.py:12
  73.7 44.1 %collective-permute-start.4 = (s32[256]{0:T(256)S(1)}, s32[256]{0:T(256)S(1)}, u32[]{:S(2)}, u32[]{:S(2)}) collective-permute-start(s32[256]{0:T(256)S(1)} %collective-permute-done), channel_id=1, source_target_pairs={{0,2},{2,4},{4,6},{6,8},{8,10},{10,12},{12,14},{1,3},{3,5},{5,7},{... | collective-permute-start | bytes 3080 | tf_op jit(solution)/shard_map/ppermute | solution.py:12
  78.9 39.0 %collective-permute-start.6 = (s32[256]{0:T(256)S(1)}, s32[256]{0:T(256)S(1)}, u32[]{:S(2)}, u32[]{:S(2)}) collective-permute-start(s32[256]{0:T(256)S(1)} %collective-permute-done.2), channel_id=1, source_target_pairs={{2,0},{4,2},{6,4},{8,6},{10,8},{12,10},{14,12},{3,1},{5,3},{7,5},{... | collective-permute-start | bytes 3080 | tf_op jit(solution)/shard_map/ppermute | solution.py:12
  80.2 32.4 %collective-permute-start.1 = (bf16[256,768]{1,0:T(8,128)(2,1)S(1)}, bf16[256,768]{1,0:T(8,128)(2,1)S(1)}, u32[]{:S(2)}, u32[]{:S(2)}) collective-permute-start(bf16[256,768]{1,0:T(8,128)(2,1)S(1)} %scatter_custom_fusion.3), channel_id=1, source_target_pairs={{0,2},{2,4},{4,6},{6,8},{8,10},{10,12},{12,14},{1,3},{3,5},{5,7},{... | collective-permute-start | bytes 1179656 | tf_op jit(solution)/shard_map/ppermute | solution.py:12
  88.5 28.9 %collective-permute-start.7 = (bf16[256,768]{1,0:T(8,128)(2,1)S(1)}, bf16[256,768]{1,0:T(8,128)(2,1)S(1)}, u32[]{:S(2)}, u32[]{:S(2)}) collective-permute-start(bf16[256,768]{1,0:T(8,128)(2,1)S(1)} %collective-permute-done.3), channel_id=1, source_target_pairs={{2,0},{4,2},{6,4},{8,6},{10,8},{12,10},{14,12},{3,1},{5,3},{7,5},{... | collective-permute-start | bytes 1179656 | tf_op jit(solution)/shard_map/ppermute | solution.py:12
  112.7 15.5 %collective-permute-start.5 = (bf16[256,768]{1,0:T(8,128)(2,1)S(1)}, bf16[256,768]{1,0:T(8,128)(2,1)S(1)}, u32[]{:S(2)}, u32[]{:S(2)}) collective-permute-start(bf16[256,768]{1,0:T(8,128)(2,1)S(1)} %collective-permute-done.1), channel_id=1, source_target_pairs={{0,2},{2,4},{4,6},{6,8},{8,10},{10,12},{12,14},{1,3},{3,5},{5,7},{... | collective-permute-start | bytes 1179656 | tf_op jit(solution)/shard_map/ppermute | solution.py:12
  129.5 11.1 %all-to-all-start.2 = ((f32[8,1,64]{2,1,0:T(1,128)}), f32[8,1,64]{2,1,0:T(1,128)S(1)}, u32[]{:S(2)}, u32[]{:S(2)}) async-start(f32[8,1,64]{2,1,0:T(1,128)} %max.65), calls=%async_computation.2 | async-start | bytes 8192 | tf_op jit(solution)/shard_map/all_to_all | solution.py:103
Sparse Core Ops, SparseCore 0:
  41.4 8.7 all-gather.4
  52.5 89.2 all-gather.6
